TPU v7x, 256 devices: a whole 4x4x8 slice. The times are simulated.
256 devices in a mesh: seq: 32 (over x, z), batch: 8 (over y, core).
Axes of the slice: x: 4, y: 4, z: 8, core: 2. Of those that a mesh axis runs over, the one named last changes fastest.
Arguments:
- hidden: bfloat16 [16, 8192, 4096], P('batch', None, 'seq')
- gain: float32 [4096], P('seq'), may hold values from 0.5 to 1.5
- value_weight: float32 [4096], P('seq'), may hold values from -0.09375 to 0.09375
- rewards: float32 [16, 8192], P('batch', 'seq'), may hold values from -1.5 to 1.5
- reward_mask: int32 [16, 8192], P('batch', 'seq'), may hold values 0 or 1
- lengths: int32 [16], P('batch'), may hold values from 2048 to 8192
- horizon: float32 [16], P('batch'), may hold values from 24 to 65536
Outputs:
- advantages: float32 [16, 8192], P(None, ('seq', 'batch'))
- returns: float32 [16, 8192], P(None, ('seq', 'batch'))
All inputs are finite; a program needn't handle non-finite values. No bound on the sum of `reward_mask` on one device may be relied on, other than what follows from the above.
Results may differ from a plain program's by a relative error of at most 0.0003.
Values may be sent and summed in bfloat16 or wider, within the bound.
A program may use at most 64 MiB of HBM per device.

v0:
```python
import jax
import jax.numpy as jnp
from jax import lax
from jax.sharding import Mesh
from jax.sharding import PartitionSpec as P

D = 4096
SEQ = ("seq_0", "seq_1")
SEQ_BATCH = ("seq_0", "seq_1", "batch_0", "batch_1")
BATCH = ("batch_0", "batch_1")
EPS = 1e-05


def cut_along(array, dim, devices):
    dims = array.shape
    blocks = array.reshape(*dims[:dim], devices, dims[dim] // devices, *dims[dim + 1 :])
    return jnp.moveaxis(blocks, dim, 0)


def sent_and_summed(array, axis, dim):
    devices = lax.axis_size(axis)
    blocks = lax.all_to_all(cut_along(array, dim, devices), axis, 0, 0, tiled=True)
    return jnp.sum(blocks, axis=0)


def side_by_side(arrays, axis, dim, along):
    widths = [a.shape[along] for a in arrays]
    both = jnp.concatenate(arrays, axis=along)
    whole = sent_and_summed(both, axis, dim)
    return tuple(jnp.split(whole, [sum(widths[:k]) for k in range(1, len(widths))], axis=along))


def from_behind(value, axis, steps):
    count = lax.axis_size(axis)
    initial, last = (max(0, -steps), min(count, count - steps))
    return lax.ppermute(value, axis, [(source, source + steps) for source in range(initial, last)])


def sent_to_all(array, axis):
    devices = lax.axis_size(axis)
    return lax.all_to_all(
        jnp.broadcast_to(array[None], (devices, *array.shape)), axis, 0, 0, tiled=True
    )


def gathered_once(array, axis):
    leaves = jax.tree.leaves(array)
    turns = sorted(range(len(leaves)), key=lambda k: -leaves[k].size)
    width = (1, *leaves[turns[0]].shape)[-1]
    lines = [
        jnp.pad(leaves[k].reshape(-1), (0, -leaves[k].size % width)).reshape(-1, width)
        for k in turns
    ]
    both, at, found = (sent_to_all(jnp.concatenate(lines), axis), 0, {})
    for k, line in zip(turns, lines):
        slab = both[:, at : at + len(line)].reshape(len(both), -1)
        found[k] = slab[:, : leaves[k].size].reshape(-1, *leaves[k].shape)
        at += len(line)
    numbers = iter(range(len(leaves)))
    return jax.tree.map(lambda _: found[next(numbers)], array)


def joined_by_halves(pieces, combine):
    while len(jax.tree.leaves(pieces)[0]) > 1:
        pieces = jax.vmap(combine)(
            *(jax.tree.map(lambda part: part[side::2], pieces) for side in (0, 1))
        )
    return jax.tree.map(lambda part: part[0], pieces)


def prefix(array, axis, combine, identity):
    devices, position = (lax.axis_size(axis), lax.axis_index(axis))
    passed = jnp.arange(devices) > position

    def kept(part, zero, own):
        part = jnp.where(
            passed.reshape(-1, *(1 for _ in own.shape)), part, jnp.asarray(zero, own.dtype)
        )
        return part[::-1]

    pieces = gathered_once(array, axis)
    return joined_by_halves(jax.tree.map(kept, pieces, identity, array), combine)


def one_axis_at_a_time(array, axes):
    for axis in axes:
        array = lax.psum(array, axis)
    return array


def per_device(hidden, gain, value_weight, rewards, reward_mask, lengths, horizon):
    my_index = lax.axis_index(SEQ)
    block = rewards.shape[1]
    wide_rows = hidden.astype(jnp.float32)
    part_squares = jnp.sum(wide_rows * wide_rows, -1)
    part_projected = jnp.sum(wide_rows * (gain * value_weight), -1)
    squares, projected = side_by_side((part_squares, part_projected), SEQ, 1, 0)
    values = projected * lax.rsqrt(squares / D + EPS)
    positions = my_index * block + jnp.arange(block, dtype=jnp.int32)
    valid = (positions[None, :] < lengths[:, None]).astype(jnp.float32)
    next_valid = (positions[None, :] + 1 < lengths[:, None]).astype(jnp.float32)
    following = from_behind(values[:, 0], SEQ, -1)
    next_values = jnp.concatenate([values[:, 1:], following[:, None]], 1)
    delta = (rewards * reward_mask.astype(jnp.float32) + next_valid * next_values - values) * valid
    log_decay = -1.0 / horizon
    offsets = jnp.arange(block, dtype=jnp.int32)
    distance = (offsets[None, :] - offsets[:, None]).astype(jnp.float32)
    upper_mask = distance >= 0.0
    powers = jnp.where(
        upper_mask[None], jnp.exp(jnp.maximum(distance, 0.0)[None] * log_decay[:, None, None]), 0.0
    )
    local_gae = jnp.einsum("rtk,rk->rt", powers, delta, precision=lax.Precision.HIGHEST)
    tail_decay = jnp.exp((block - offsets).astype(jnp.float32)[None, :] * log_decay[:, None])
    start_value = local_gae[:, 0]
    block_decay = jnp.exp(block * log_decay)

    def compose(earlier, later):
        return (later[0] + later[1] * earlier[0], later[1] * earlier[1])

    carry_in, _ = prefix(
        (start_value, block_decay),
        SEQ,
        compose,
        (jnp.zeros_like(start_value), jnp.ones_like(block_decay)),
    )
    gae = local_gae + tail_decay * carry_in[:, None]
    returns = (gae + values) * valid
    count, first, second = (
        one_axis_at_a_time(jnp.sum(valid), SEQ_BATCH),
        one_axis_at_a_time(jnp.sum(gae), SEQ_BATCH),
        one_axis_at_a_time(jnp.sum(gae * gae), SEQ_BATCH),
    )
    mean = first / count
    var = jnp.maximum(second / count - mean * mean, 1.0)
    whitened = (gae - mean) * valid * lax.rsqrt(var)
    out_adv, out_returns = (
        lax.all_to_all(whitened, BATCH, split_axis=1, concat_axis=0, tiled=True),
        lax.all_to_all(returns, BATCH, split_axis=1, concat_axis=0, tiled=True),
    )
    return (out_adv, out_returns)


def solution(mesh):
    finer = Mesh(mesh.devices.reshape(4, 8, 4, 2), ("seq_0", "seq_1", "batch_0", "batch_1"))
    placed = (P(BATCH, None, SEQ), P(SEQ), P(SEQ), P(BATCH, SEQ), P(BATCH, SEQ), P(BATCH), P(BATCH))
    return jax.shard_map(
        per_device,
        mesh=finer,
        in_specs=placed,
        out_specs=(P(None, SEQ_BATCH), P(None, SEQ_BATCH)),
        check_vma=False,
    )
```

profile of v0, /device:TPU:1, one launch (start us, length us, event | category | flops | bytes accessed | tf_op | source)
XLA Modules:
  0.0 118.5 jit_solution(17248735630217335933)
XLA Ops:
  0.6 0.0 copy-start.3
  0.6 0.0 copy-start.1
  0.7 0.0 copy-start.2
  0.7 0.0 copy-start
  0.7 0.7 mul.124
  1.4 6.7 %fusion = (f32[2,8192]{1,0:T(2,128)S(1)}, f32[2,8192]{1,0:T(2,128)S(1)}) fusion(bf16[2,8192,128]{2,1,0:T(8,128)(2,1)} %param.7, f32[128]{0:T(128)S(1)} %mul.124), kind=kLoop, calls=%fused_computation.2 | loop fusion | flops 10452992 | bytes 4325888 | tf_op jit(solution)/shard_map/reduce_sum | solution.py:95
  8.0 0.7 pad_maximum_fusion
  8.7 11.9 %all-to-all-start = ((f32[32,4,256]{2,1,0:T(4,128)}), f32[32,4,256]{2,1,0:T(4,128)S(1)}, u32[]{:S(2)}, u32[]{:S(2)}) async-start(f32[32,4,256]{2,1,0:T(4,128)} %bitcast.1), calls=%async_computation | async-start | bytes 262144 | tf_op jit(solution)/shard_map/all_to_all | solution.py:22
  20.6 0.1 convert_compare_fusion
  20.7 0.0 copy-done.3
  20.8 9.0 %all-to-all-done = f32[32,4,256]{2,1,0:T(4,128)S(1)} async-done(((f32[32,4,256]{2,1,0:T(4,128)}), f32[32,4,256]{2,1,0:T(4,128)S(1)}, u32[]{:S(2)}, u32[]{:S(2)}) %all-to-all-start) | async-done | bytes 131104 | tf_op jit(solution)/shard_map/all_to_all | solution.py:22
  29.8 0.1 slice_reduce_fusion.1
  29.9 0.1 slice.115
  30.0 1.3 %collective-permute-start = (f32[2]{0:T(128)S(1)}, f32[2]{0:T(128)S(1)}, u32[]{:S(2)}, u32[]{:S(2)}) collective-permute-start(f32[2]{0:T(128)S(1)} %slice_reduce_fusion.1), channel_id=1, source_target_pairs={{8,0},{16,8},{24,16},{32,24},{40,32},{48,40},{56,48},{64,56},{72,6... | collective-permute-start | bytes 32 | tf_op jit(solution)/shard_map/ppermute | solution.py:36
  31.3 3.0 %collective-permute-done = f32[2]{0:T(128)S(1)} collective-permute-done((f32[2]{0:T(128)S(1)}, f32[2]{0:T(128)S(1)}, u32[]{:S(2)}, u32[]{:S(2)}) %collective-permute-start) | collective-permute-done | bytes 40 | tf_op jit(solution)/shard_map/ppermute | solution.py:36
  34.3 0.1 copy.15
  34.4 0.0 copy-done.1
  34.4 0.0 copy-done.2
  34.4 0.1 fusion.18
  34.5 0.7 fusion.2
  35.2 0.1 slice_reduce_fusion
  35.3 0.6 broadcast_in_dim.55
  35.9 5.2 %all-to-all-start.1 = ((f32[32,2,2]{2,1,0:T(2,128)}), f32[32,2,2]{2,1,0:T(2,128)S(1)}, u32[]{:S(2)}, u32[]{:S(2)}) async-start(f32[32,2,2]{2,1,0:T(2,128)} %broadcast_in_dim.55), calls=%async_computation.1 | async-start | bytes 65536 | tf_op jit(solution)/shard_map/all_to_all | solution.py:41
  41.1 8.8 %all-to-all-done.1 = f32[32,2,2]{2,1,0:T(2,128)S(1)} async-done(((f32[32,2,2]{2,1,0:T(2,128)}), f32[32,2,2]{2,1,0:T(2,128)S(1)}, u32[]{:S(2)}, u32[]{:S(2)}) %all-to-all-start.1) | async-done | bytes 544 | tf_op jit(solution)/shard_map/all_to_all | solution.py:41
  49.9 0.1 copy.16
  50.0 0.1 copy.17
  50.1 0.1 slice.99
  50.2 0.1 slice.94
  50.3 0.1 slice.91
  50.4 0.1 slice.96
  50.5 0.1 slice.100
  50.6 0.1 slice.92
  50.7 0.1 slice.95
  50.8 0.1 slice.97
  50.9 0.1 slice.101
  51.0 0.1 slice.104
  51.1 0.1 slice.102
  51.2 0.1 slice.98
  51.3 0.1 slice.103
  51.4 0.1 slice.106
  51.5 0.1 slice.105
  51.6 0.1 slice.108
  51.7 0.1 slice.107
  51.8 0.1 slice.110
  51.9 0.1 slice.109
  52.0 0.1 slice.112
  52.1 0.2 add_reduce_fusion
  52.3 0.7 compare_select_fusion
  53.0 0.6 fusion.20
  53.6 7.6 %all-reduce.2 = (f32[]{:T(128)}, f32[]{:T(128)}, f32[]{:T(128)}) all-reduce(f32[]{:T(128)} %get-tuple-element.5, f32[]{:T(128)} %get-tuple-element.24, f32[]{:T(128)} %get-tuple-element.4), channel_id=1, replica_groups=mesh['seq_0'=4,'seq_1'=8,'batch_0'=4,'batch_1'=2] {'seq_0'}, use_global_device_ids=true, to_apply=%region_14.15 | all-reduce | flops 3 | bytes 24 | tf_op jit(solution)/shard_map/psum | solution.py:87
  61.1 11.8 %all-reduce = (f32[]{:T(128)}, f32[]{:T(128)}, f32[]{:T(128)}) all-reduce(f32[]{:T(128)} %get-tuple-element.12, f32[]{:T(128)} %get-tuple-element.13, f32[]{:T(128)} %get-tuple-element.14), channel_id=1, replica_groups=mesh['seq_0'=4,'seq_1'=8,'batch_0'=4,'batch_1'=2] {'seq_1'}, use_global_device_ids=true, to_apply=%region_15.16 | all-reduce | flops 3 | bytes 24 | tf_op jit(solution)/shard_map/psum | solution.py:87
  72.9 9.7 %all-reduce.1 = (f32[]{:T(128)}, f32[]{:T(128)}, f32[]{:T(128)}) all-reduce(f32[]{:T(128)} %get-tuple-element.6, f32[]{:T(128)} %get-tuple-element.7, f32[]{:T(128)} %get-tuple-element.8), channel_id=1, replica_groups=mesh['seq_0'=4,'seq_1'=8,'batch_0'=4,'batch_1'=2] {'batch_0'}, use_global_device_ids=true, to_apply=%region_16.17 | all-reduce | flops 3 | bytes 24 | tf_op jit(solution)/shard_map/psum | solution.py:87
  82.6 14.5 %all-reduce.3 = (f32[]{:T(128)}, f32[]{:T(128)}, f32[]{:T(128)}) all-reduce(f32[]{:T(128)} %get-tuple-element.9, f32[]{:T(128)} %get-tuple-element.10, f32[]{:T(128)} %get-tuple-element.11), channel_id=1, replica_groups=mesh['seq_0'=4,'seq_1'=8,'batch_0'=4,'batch_1'=2] {'batch_1'}, use_global_device_ids=true, to_apply=%region_17.18 | all-reduce | flops 3 | bytes 24 | tf_op jit(solution)/shard_map/psum | solution.py:87
  99.8 0.1 fusion.13
  99.9 0.1 all_to_all.36
  99.9 0.6 copy.18
  100.6 3.6 %all-to-all-start.2 = ((f32[2,8,32]{2,0,1:T(2,128)}), f32[2,8,32]{2,0,1:T(2,128)S(1)}, u32[]{:S(2)}, u32[]{:S(2)}) async-start(f32[2,8,32]{2,0,1:T(2,128)} %copy.18), calls=%async_computation.2 | async-start | bytes 16384 | tf_op jit(solution)/shard_map/all_to_all | solution.py:137
  104.1 0.1 all_to_all.40
  104.2 0.6 copy.19
  104.8 4.0 %all-to-all-done.2 = f32[2,8,32]{2,0,1:T(2,128)S(1)} async-done(((f32[2,8,32]{2,0,1:T(2,128)}), f32[2,8,32]{2,0,1:T(2,128)S(1)}, u32[]{:S(2)}, u32[]{:S(2)}) %all-to-all-start.2) | async-done | bytes 2080 | tf_op jit(solution)/shard_map/all_to_all | solution.py:137
  108.8 3.9 %all-to-all-start.3 = ((f32[2,8,32]{2,0,1:T(2,128)}), f32[2,8,32]{2,0,1:T(2,128)S(1)}, u32[]{:S(2)}, u32[]{:S(2)}) async-start(f32[2,8,32]{2,0,1:T(2,128)} %copy.19), calls=%async_computation.3 | async-start | bytes 16384 | tf_op jit(solution)/shard_map/all_to_all | solution.py:138
  112.7 4.6 %all-to-all-done.3 = f32[2,8,32]{2,0,1:T(2,128)S(1)} async-done(((f32[2,8,32]{2,0,1:T(2,128)}), f32[2,8,32]{2,0,1:T(2,128)S(1)}, u32[]{:S(2)}, u32[]{:S(2)}) %all-to-all-start.3) | async-done | bytes 2080 | tf_op jit(solution)/shard_map/all_to_all | solution.py:138
  117.4 0.6 copy.31
  118.0 0.6 copy.32
  (16 shorter events, 0.2 us)
Async XLA Ops:
  0.6 20.1 %copy-start.3 = (f32[2]{0:T(128)S(1)}, f32[2]{0:T(128)}, u32[]{:S(2)}) copy-start(f32[2]{0:T(128)} %param.13) | copy-start | bytes 28
  0.6 33.8 %copy-start.1 = (f32[2,256]{1,0:T(2,128)S(1)}, f32[2,256]{1,0:T(2,128)}, u32[]{:S(2)}) copy-start(f32[2,256]{1,0:T(2,128)} %param.10) | copy-start | bytes 6148
  0.7 33.7 %copy-start.2 = (s32[2,256]{1,0:T(2,128)S(1)}, s32[2,256]{1,0:T(2,128)}, u32[]{:S(2)}) copy-start(s32[2,256]{1,0:T(2,128)} %param.11) | copy-start | bytes 6148
  0.7 33.7 %copy-start = (s32[2]{0:T(128)S(1)}, s32[2]{0:T(128)}, u32[]{:S(2)}) copy-start(s32[2]{0:T(128)} %param.12) | copy-start | bytes 28
  8.7 21.0 %all-to-all-start = ((f32[32,4,256]{2,1,0:T(4,128)}), f32[32,4,256]{2,1,0:T(4,128)S(1)}, u32[]{:S(2)}, u32[]{:S(2)}) async-start(f32[32,4,256]{2,1,0:T(4,128)} %bitcast.1), calls=%async_computation | async-start | bytes 262144 | tf_op jit(solution)/shard_map/all_to_all | solution.py:22
  30.0 4.3 %collective-permute-start = (f32[2]{0:T(128)S(1)}, f32[2]{0:T(128)S(1)}, u32[]{:S(2)}, u32[]{:S(2)}) collective-permute-start(f32[2]{0:T(128)S(1)} %slice_reduce_fusion.1), channel_id=1, source_target_pairs={{8,0},{16,8},{24,16},{32,24},{40,32},{48,40},{56,48},{64,56},{72,6... | collective-permute-start | bytes 32 | tf_op jit(solution)/shard_map/ppermute | solution.py:36
  35.9 13.9 %all-to-all-start.1 = ((f32[32,2,2]{2,1,0:T(2,128)}), f32[32,2,2]{2,1,0:T(2,128)S(1)}, u32[]{:S(2)}, u32[]{:S(2)}) async-start(f32[32,2,2]{2,1,0:T(2,128)} %broadcast_in_dim.55), calls=%async_computation.1 | async-start | bytes 65536 | tf_op jit(solution)/shard_map/all_to_all | solution.py:41
  100.6 8.2 %all-to-all-start.2 = ((f32[2,8,32]{2,0,1:T(2,128)}), f32[2,8,32]{2,0,1:T(2,128)S(1)}, u32[]{:S(2)}, u32[]{:S(2)}) async-start(f32[2,8,32]{2,0,1:T(2,128)} %copy.18), calls=%async_computation.2 | async-start | bytes 16384 | tf_op jit(solution)/shard_map/all_to_all | solution.py:137
  108.8 8.6 %all-to-all-start.3 = ((f32[2,8,32]{2,0,1:T(2,128)}), f32[2,8,32]{2,0,1:T(2,128)S(1)}, u32[]{:S(2)}, u32[]{:S(2)}) async-start(f32[2,8,32]{2,0,1:T(2,128)} %copy.19), calls=%async_computation.3 | async-start | bytes 16384 | tf_op jit(solution)/shard_map/all_to_all | solution.py:138
where the time goes:
time: 119 us
  blocking collectives  43.6 us (37%)
  waiting for transfers between devices  29.3 us (25%)
  starting transfers between devices  25.8 us (22%)
  other arithmetic  9.9 us (8%)
  local copies, waits for them, and re-layouts  5.74 us (5%)
  between operations  3.44 us (3%)
    psum x4, blocking collectives, one_axis_at_a_time(): array = lax.psum(array, axis)  43.6 us
    all_to_all x1, starting transfers between devices, sent_and_summed(): lax.all_to_all(cut_along(array, dim, devices), axis, 0, 0, tiled=True)  11.9 us
    all_to_all x1, waiting for transfers between devices, sent_and_summed(): lax.all_to_all(cut_along(array, dim, devices), axis, 0, 0, tiled=True)  8.98 us
    all_to_all x1, waiting for transfers between devices, sent_to_all(): lax.all_to_all(jnp.broadcast_to(array[None], (devices, *array.shape)), ax...  8.76 us
    reduce_sum x1, other arithmetic, per_device(): part_squares = jnp.sum(wide_rows * wide_rows, -1)  6.65 us
    all_to_all x1, starting transfers between devices, sent_to_all(): lax.all_to_all(jnp.broadcast_to(array[None], (devices, *array.shape)), ax...  5.16 us
    all_to_all x1, waiting for transfers between devices, per_device(): lax.all_to_all(returns, BATCH, split_axis=1, concat_axis=0, tiled=True)  4.64 us
    all_to_all x1, waiting for transfers between devices, per_device(): lax.all_to_all(whitened, BATCH, split_axis=1, concat_axis=0, tiled=True)  3.96 us
  transfers between devices with their start and end apart: 5, of which 5 were waited for; matrix products, arithmetic and copies ran while one was open for 1% of the time, Pallas kernels for 0%

commit v1 on v0

--- a/solution.py
+++ b/solution.py
@@ -84,7 +84,7 @@
 
 def one_axis_at_a_time(array, axes):
     for axis in axes:
-        array = lax.psum(array, axis)
+        array = jax.lax.all_gather(array, axis).sum(axis=0)
     return array
 
 

time: 119 us -> 143 us (1.20)
  local copies, waits for them, and re-layouts: 5.74 us -> 25.1 us
  other arithmetic: 9.9 us -> 17.5 us
  blocking collectives: 43.6 us -> 40.9 us
    psum x4 -> x0, blocking collectives: 43.6 us -> none  [one_axis_at_a_time(): array = lax.psum(array, axis)]
    unnamed x0 -> x4, blocking collectives: none -> 40.9 us
    unnamed x10 -> x46, local copies, waits for them, and re-layouts: 1.21 us -> 20.6 us
    reduce_sum x0 -> x12, other arithmetic: none -> 7.45 us  [one_axis_at_a_time(): array = jax.lax.all_gather(array, axis).sum(axis=0)]
where the time goes in v1:
time: 143 us; the launch traced here: 142 us
  blocking collectives  40.9 us (29%)
  waiting for transfers between devices  28.7 us (20%)
  starting transfers between devices  25.8 us (18%)
  local copies, waits for them, and re-layouts  25.1 us (18%)
  other arithmetic  17.5 us (12%)
  between operations  3.6 us (3%)
    unnamed x4, blocking collectives  40.9 us
    unnamed x46, local copies, waits for them, and re-layouts  20.6 us
    all_to_all x1, starting transfers between devices, sent_and_summed(): lax.all_to_all(cut_along(array, dim, devices), axis, 0, 0, tiled=True)  11.9 us
    all_to_all x1, waiting for transfers between devices, sent_and_summed(): lax.all_to_all(cut_along(array, dim, devices), axis, 0, 0, tiled=True)  8.98 us
    all_to_all x1, waiting for transfers between devices, sent_to_all(): lax.all_to_all(jnp.broadcast_to(array[None], (devices, *array.shape)), ax...  8.13 us
    reduce_sum x12, other arithmetic, one_axis_at_a_time(): array = jax.lax.all_gather(array, axis).sum(axis=0)  7.45 us
    reduce_sum x1, other arithmetic, per_device(): part_squares = jnp.sum(wide_rows * wide_rows, -1)  6.65 us
    all_to_all x1, starting transfers between devices, sent_to_all(): lax.all_to_all(jnp.broadcast_to(array[None], (devices, *array.shape)), ax...  5.16 us
  transfers between devices with their start and end apart: 5, of which 5 were waited for; matrix products, arithmetic and copies ran while one was open for 1% of the time, Pallas kernels for 0%

profile of v1, /device:TPU:1, one launch (start us, length us, event | category | flops | bytes accessed | tf_op | source)
XLA Modules:
  0.0 142.3 jit_solution(13265880173990722360)
XLA Ops:
  0.7 0.7 mul.124
  1.4 6.7 %fusion = (f32[2,8192]{1,0:T(2,128)S(1)}, f32[2,8192]{1,0:T(2,128)S(1)}) fusion(bf16[2,8192,128]{2,1,0:T(8,128)(2,1)} %param.7, f32[128]{0:T(128)S(1)} %mul.124), kind=kLoop, calls=%fused_computation.2 | loop fusion | flops 10452992 | bytes 4325888 | tf_op jit(solution)/shard_map/reduce_sum | solution.py:95
  8.1 0.7 pad_maximum_fusion
  8.8 11.9 %all-to-all-start = ((f32[32,4,256]{2,1,0:T(4,128)}), f32[32,4,256]{2,1,0:T(4,128)S(1)}, u32[]{:S(2)}, u32[]{:S(2)}) async-start(f32[32,4,256]{2,1,0:T(4,128)} %bitcast.1), calls=%async_computation | async-start | bytes 262144 | tf_op jit(solution)/shard_map/all_to_all | solution.py:22
  20.8 9.0 %all-to-all-done = f32[32,4,256]{2,1,0:T(4,128)S(1)} async-done(((f32[32,4,256]{2,1,0:T(4,128)}), f32[32,4,256]{2,1,0:T(4,128)S(1)}, u32[]{:S(2)}, u32[]{:S(2)}) %all-to-all-start) | async-done | bytes 131104 | tf_op jit(solution)/shard_map/all_to_all | solution.py:22
  29.9 0.1 slice_reduce_fusion.1
  30.1 1.3 collective-permute-start
  31.4 3.0 %collective-permute-done = f32[2]{0:T(128)S(1)} collective-permute-done((f32[2]{0:T(128)S(1)}, f32[2]{0:T(128)S(1)}, u32[]{:S(2)}, u32[]{:S(2)}) %collective-permute-start) | collective-permute-done | bytes 40 | tf_op jit(solution)/shard_map/ppermute | solution.py:36
  34.5 0.7 fusion.2
  35.2 0.1 slice_reduce_fusion
  35.4 0.6 broadcast_in_dim.55
  36.0 5.2 %all-to-all-start.1 = ((f32[32,2,2]{2,1,0:T(2,128)}), f32[32,2,2]{2,1,0:T(2,128)S(1)}, u32[]{:S(2)}, u32[]{:S(2)}) async-start(f32[32,2,2]{2,1,0:T(2,128)} %broadcast_in_dim.55), calls=%async_computation.1 | async-start | bytes 65536 | tf_op jit(solution)/shard_map/all_to_all | solution.py:41
  41.2 0.6 dynamic-slice
  41.8 8.1 %all-to-all-done.1 = f32[32,2,2]{2,1,0:T(2,128)S(1)} async-done(((f32[32,2,2]{2,1,0:T(2,128)}), f32[32,2,2]{2,1,0:T(2,128)S(1)}, u32[]{:S(2)}, u32[]{:S(2)}) %all-to-all-start.1) | async-done | bytes 544 | tf_op jit(solution)/shard_map/all_to_all | solution.py:41
  50.1 0.1 slice.99
  50.3 0.1 slice.94
  50.4 0.1 slice.91
  50.5 0.1 slice.96
  50.6 0.1 slice.100
  51.0 0.1 slice.101
  51.3 0.1 slice.98
  51.8 0.1 slice.107
  52.1 0.2 add_reduce_fusion
  52.3 0.7 compare_select_fusion
  53.0 0.7 fusion.20
  53.7 1.4 dynamic-update-slice
  55.1 1.4 %dynamic-update-slice.8 = f32[4]{0:T(128)S(1)} dynamic-update-slice(f32[4]{0:T(128)S(1)} %broadcast.69.clone.1, f32[1]{0:T(128)} %bitcast.20, u32[]{:T(128)} %bitcast.9) | dynamic-update-slice | bytes 12
  56.5 1.4 dynamic-update-slice.4
  57.9 0.6 dynamic-slice.1
  58.5 6.8 %all-reduce.14 = (f32[4]{0:T(128)S(1)}, f32[4]{0:T(128)S(1)}, f32[4]{0:T(128)S(1)}) all-reduce(f32[4]{0:T(128)S(1)} %dynamic-update-slice.8, f32[4]{0:T(128)S(1)} %dynamic-update-slice.4, f32[4]{0:T(128)S(1)} %dynamic-update-slice), channel_id=1, replica_groups=mesh['seq_0'=4,'seq_1'=8,'batch_0'=4,'batch_1'=2] {'seq_0'}, use_global_device_ids=true, to_apply=%add.8 | all-reduce | flops 12 | bytes 96
  65.4 0.7 reduce_sum.166
  66.0 0.6 reduce_sum.171
  66.6 1.4 %dynamic-update-slice.1 = f32[8]{0:T(128)S(1)} dynamic-update-slice(f32[8]{0:T(128)S(1)} %broadcast.68.clone.2, f32[1]{0:T(128)} %bitcast.10, u32[]{:T(128)} %bitcast.11) | dynamic-update-slice | bytes 12
  68.1 1.4 dynamic-update-slice.5
  69.5 0.6 reduce_sum.176
  70.1 1.4 dynamic-update-slice.9
  71.5 0.6 dynamic-slice.2
  72.1 11.1 %all-reduce.12 = (f32[8]{0:T(128)S(1)}, f32[8]{0:T(128)S(1)}, f32[8]{0:T(128)S(1)}) all-reduce(f32[8]{0:T(128)S(1)} %dynamic-update-slice.9, f32[8]{0:T(128)S(1)} %dynamic-update-slice.5, f32[8]{0:T(128)S(1)} %dynamic-update-slice.1), channel_id=1, replica_groups=mesh['seq_0'=4,'seq_1'=8,'batch_0'=4,'batch_1'=2] {'seq_1'}, use_global_device_ids=true, to_apply=%add.9 | all-reduce | flops 24 | bytes 192
  83.2 0.7 reduce_sum.167
  83.8 0.6 reduce_sum.172
  84.4 1.4 %dynamic-update-slice.2 = f32[4]{0:T(128)S(1)} dynamic-update-slice(f32[4]{0:T(128)S(1)} %broadcast.69.clone.5, f32[1]{0:T(128)} %bitcast.12, u32[]{:T(128)} %bitcast.13) | dynamic-update-slice | bytes 12
  85.9 1.4 dynamic-update-slice.6
  87.3 0.6 reduce_sum.177
  87.9 1.4 dynamic-update-slice.10
  89.3 0.6 dynamic-slice.3
  89.9 8.7 %all-reduce.13 = (f32[4]{0:T(128)S(1)}, f32[4]{0:T(128)S(1)}, f32[4]{0:T(128)S(1)}) all-reduce(f32[4]{0:T(128)S(1)} %dynamic-update-slice.10, f32[4]{0:T(128)S(1)} %dynamic-update-slice.6, f32[4]{0:T(128)S(1)} %dynamic-update-slice.2), channel_id=1, replica_groups=mesh['seq_0'=4,'seq_1'=8,'batch_0'=4,'batch_1'=2] {'batch_0'}, use_global_device_ids=true, to_apply=%add.10 | all-reduce | flops 12 | bytes 96
  98.6 0.7 reduce_sum.168
  99.3 0.6 reduce_sum.173
  99.9 1.4 %dynamic-update-slice.3 = f32[2]{0:T(128)S(1)} dynamic-update-slice(f32[2]{0:T(128)S(1)} %broadcast.70.clone.2, f32[1]{0:T(128)} %bitcast.14, u32[]{:T(128)} %bitcast.15) | dynamic-update-slice | bytes 12
  101.3 1.4 dynamic-update-slice.7
  102.7 0.6 reduce_sum.178
  103.3 1.4 dynamic-update-slice.11
  104.7 14.3 %all-reduce.15 = (f32[2]{0:T(128)S(1)}, f32[2]{0:T(128)S(1)}, f32[2]{0:T(128)S(1)}) all-reduce(f32[2]{0:T(128)S(1)} %dynamic-update-slice.11, f32[2]{0:T(128)S(1)} %dynamic-update-slice.7, f32[2]{0:T(128)S(1)} %dynamic-update-slice.3), channel_id=1, replica_groups=mesh['seq_0'=4,'seq_1'=8,'batch_0'=4,'batch_1'=2] {'batch_1'}, use_global_device_ids=true, to_apply=%add.11 | all-reduce | flops 6 | bytes 48
  119.0 0.6 reduce_sum.169
  119.6 0.6 reduce_sum.174
  121.5 0.6 reduce_sum.179
  123.7 0.6 copy.18
  124.3 3.6 %all-to-all-start.2 = ((f32[2,8,32]{2,0,1:T(2,128)}), f32[2,8,32]{2,0,1:T(2,128)S(1)}, u32[]{:S(2)}, u32[]{:S(2)}) async-start(f32[2,8,32]{2,0,1:T(2,128)} %copy.18), calls=%async_computation.2 | async-start | bytes 16384 | tf_op jit(solution)/shard_map/all_to_all | solution.py:137
  127.9 0.6 copy.19
  128.6 4.0 %all-to-all-done.2 = f32[2,8,32]{2,0,1:T(2,128)S(1)} async-done(((f32[2,8,32]{2,0,1:T(2,128)}), f32[2,8,32]{2,0,1:T(2,128)S(1)}, u32[]{:S(2)}, u32[]{:S(2)}) %all-to-all-start.2) | async-done | bytes 2080 | tf_op jit(solution)/shard_map/all_to_all | solution.py:137
  132.5 3.9 %all-to-all-start.3 = ((f32[2,8,32]{2,0,1:T(2,128)}), f32[2,8,32]{2,0,1:T(2,128)S(1)}, u32[]{:S(2)}, u32[]{:S(2)}) async-start(f32[2,8,32]{2,0,1:T(2,128)} %copy.19), calls=%async_computation.3 | async-start | bytes 16384 | tf_op jit(solution)/shard_map/all_to_all | solution.py:138
  136.4 4.6 %all-to-all-done.3 = f32[2,8,32]{2,0,1:T(2,128)S(1)} async-done(((f32[2,8,32]{2,0,1:T(2,128)}), f32[2,8,32]{2,0,1:T(2,128)S(1)}, u32[]{:S(2)}, u32[]{:S(2)}) %all-to-all-start.3) | async-done | bytes 2080 | tf_op jit(solution)/shard_map/all_to_all | solution.py:138
  141.1 0.6 copy.56
  141.7 0.6 copy.57
  (64 shorter events, 2.1 us)
Async XLA Ops:
  0.6 40.6 %copy-start.7 = (u32[256]{0:T(256)S(1)}, u32[256]{0:T(256)}, u32[]{:S(2)}) copy-start(u32[256]{0:T(256)} %constant.45) | copy-start | bytes 3076
  0.6 57.3 %copy-start.6 = (u32[256]{0:T(256)S(1)}, u32[256]{0:T(256)}, u32[]{:S(2)}) copy-start(u32[256]{0:T(256)} %constant.50) | copy-start | bytes 3076
  0.7 70.8 %copy-start.5 = (u32[256]{0:T(256)S(1)}, u32[256]{0:T(256)}, u32[]{:S(2)}) copy-start(u32[256]{0:T(256)} %constant.55) | copy-start | bytes 3076
  0.7 88.6 %copy-start.4 = (u32[256]{0:T(256)S(1)}, u32[256]{0:T(256)}, u32[]{:S(2)}) copy-start(u32[256]{0:T(256)} %constant.60) | copy-start | bytes 3076
  0.7 20.1 %copy-start.3 = (f32[2]{0:T(128)S(1)}, f32[2]{0:T(128)}, u32[]{:S(2)}) copy-start(f32[2]{0:T(128)} %param.13) | copy-start | bytes 28
  0.7 33.8 %copy-start.1 = (f32[2,256]{1,0:T(2,128)S(1)}, f32[2,256]{1,0:T(2,128)}, u32[]{:S(2)}) copy-start(f32[2,256]{1,0:T(2,128)} %param.10) | copy-start | bytes 6148
  0.7 33.8 %copy-start.2 = (s32[2,256]{1,0:T(2,128)S(1)}, s32[2,256]{1,0:T(2,128)}, u32[]{:S(2)}) copy-start(s32[2,256]{1,0:T(2,128)} %param.11) | copy-start | bytes 6148
  0.7 33.8 %copy-start = (s32[2]{0:T(128)S(1)}, s32[2]{0:T(128)}, u32[]{:S(2)}) copy-start(s32[2]{0:T(128)} %param.12) | copy-start | bytes 28
  8.8 21.0 %all-to-all-start = ((f32[32,4,256]{2,1,0:T(4,128)}), f32[32,4,256]{2,1,0:T(4,128)S(1)}, u32[]{:S(2)}, u32[]{:S(2)}) async-start(f32[32,4,256]{2,1,0:T(4,128)} %bitcast.1), calls=%async_computation | async-start | bytes 262144 | tf_op jit(solution)/shard_map/all_to_all | solution.py:22
  30.1 4.3 %collective-permute-start = (f32[2]{0:T(128)S(1)}, f32[2]{0:T(128)S(1)}, u32[]{:S(2)}, u32[]{:S(2)}) collective-permute-start(f32[2]{0:T(128)S(1)} %slice_reduce_fusion.1), channel_id=1, source_target_pairs={{8,0},{16,8},{24,16},{32,24},{40,32},{48,40},{56,48},{64,56},{72,6... | collective-permute-start | bytes 32 | tf_op jit(solution)/shard_map/ppermute | solution.py:36
  36.0 13.9 %all-to-all-start.1 = ((f32[32,2,2]{2,1,0:T(2,128)}), f32[32,2,2]{2,1,0:T(2,128)S(1)}, u32[]{:S(2)}, u32[]{:S(2)}) async-start(f32[32,2,2]{2,1,0:T(2,128)} %broadcast_in_dim.55), calls=%async_computation.1 | async-start | bytes 65536 | tf_op jit(solution)/shard_map/all_to_all | solution.py:41
  124.3 8.2 %all-to-all-start.2 = ((f32[2,8,32]{2,0,1:T(2,128)}), f32[2,8,32]{2,0,1:T(2,128)S(1)}, u32[]{:S(2)}, u32[]{:S(2)}) async-start(f32[2,8,32]{2,0,1:T(2,128)} %copy.18), calls=%async_computation.2 | async-start | bytes 16384 | tf_op jit(solution)/shard_map/all_to_all | solution.py:137
  132.5 8.6 %all-to-all-start.3 = ((f32[2,8,32]{2,0,1:T(2,128)}), f32[2,8,32]{2,0,1:T(2,128)S(1)}, u32[]{:S(2)}, u32[]{:S(2)}) async-start(f32[2,8,32]{2,0,1:T(2,128)} %copy.19), calls=%async_computation.3 | async-start | bytes 16384 | tf_op jit(solution)/shard_map/all_to_all | solution.py:138
